TPU v7x, 32 devices: a whole 2x2x4 slice. The times are simulated.
32 devices in a mesh: row: 2 (over y), col: 4 (over x, core), rep: 4 (over z).
Axes of the slice: x: 2, y: 2, z: 4, core: 2. Of those that a mesh axis runs over, the one named last changes fastest.
Arguments:
- hidden: bfloat16 [512, 7168], P('rep'), may hold values from -6 to 6
- train_weight: bfloat16 [7168, 16384], P(('rep', 'row'), 'col'), may hold values from -0.0625 to 0.0625
- shard_order: int32 [4, 4, 2], replicated, may hold values from 0 to 1, each once within a row
Outputs:
- served_weight: bfloat16 [7168, 16384], P(None, ('col', 'row'))
- projected: float32 [512, 16384], P('rep', ('col', 'row'))
Inputs may be any that keep to these rules, and one draw needn't show every extreme that they name: Each shard_order[c, k] is a permutation of 0 to 1.
All inputs are finite; a program needn't handle non-finite values.
Results may differ from a plain program's by a relative error of at most 0.001.
Values may be sent and summed in bfloat16 or wider, within the bound.
A program may use at most 128 MiB of HBM per device.

v0:
```python
import functools

import jax
import jax.numpy as jnp
from jax import lax
from jax.experimental import pallas as pl
from jax.experimental.pallas import tpu as pltpu
from jax.sharding import PartitionSpec as P

MESH = pl.DeviceIdType.MESH
LANES = 128
VMEM_LIMIT = 8 * 1024 * 1024


def order_kernel(order_ref, tile_ref, out_ref, sem):
    _, sub_count, row_count = order_ref.shape
    c = lax.axis_index("col")
    piece_cols = out_ref.shape[2]
    sub_cols = piece_cols // sub_count
    copies = []
    for s in range(row_count):
        for k in range(sub_count):
            start = pl.multiple_of(order_ref[c, k, s] * piece_cols + k * sub_cols, LANES)
            copies.append(
                pltpu.make_async_copy(
                    tile_ref.at[:, pl.ds(start, sub_cols)],
                    out_ref.at[s, :, pl.ds(k * sub_cols, sub_cols)],
                    sem.at[s * sub_count + k],
                )
            )
    for copy in copies:
        copy.start()
    for copy in copies:
        copy.wait()


def ordered_pieces(tile, shard_order):
    _, sub_count, row_count = shard_order.shape
    rows_tile, cols_tile = tile.shape
    piece_cols = cols_tile // row_count
    sub_cols = piece_cols // sub_count
    if sub_cols % LANES == 0:
        return pl.pallas_call(
            order_kernel,
            out_shape=pltpu.VMEM((row_count, rows_tile, piece_cols), tile.dtype),
            in_specs=[
                pl.BlockSpec(memory_space=pltpu.SMEM),
                pl.BlockSpec(memory_space=pltpu.HBM),
            ],
            out_specs=pl.BlockSpec(memory_space=pltpu.VMEM),
            scratch_shapes=[pltpu.SemaphoreType.DMA((row_count * sub_count,))],
            compiler_params=pltpu.CompilerParams(vmem_limit_bytes=VMEM_LIMIT),
        )(shard_order, pltpu.with_memory_space_constraint(tile, pltpu.HBM))
    my_order = lax.dynamic_index_in_dim(shard_order, lax.axis_index("col"), 0, keepdims=False)
    blocks = tile.reshape(rows_tile, row_count, sub_count, sub_cols)
    pieces = []
    for s in range(row_count):
        piece = blocks[:, 0]
        for j in range(1, row_count):
            piece = jnp.where((my_order[:, s] == j)[None, :, None], blocks[:, j], piece)
        pieces.append(piece.reshape(rows_tile, piece_cols))
    return jnp.stack(pieces)


def gather_kernel(n_row, n_rep, chunks, own_ref, hidden_ref, out_ref, projected_ref, y_send, y_recv, z_recv, up_send, down_send):
    r, c, z = lax.axis_index("row"), lax.axis_index("col"), lax.axis_index("rep")
    rows_tile = own_ref.shape[1]
    rows = rows_tile // chunks
    has_up, has_down = z < n_rep - 1, z > 0
    above = (r, c, jnp.minimum(z + 1, n_rep - 1))
    below = (r, c, jnp.maximum(z - 1, 0))
    per_level = n_row * chunks

    barrier = pltpu.get_barrier_semaphore()
    for t in range(1, n_row):
        pl.semaphore_signal(barrier, inc=1, device_id=(lax.rem(r + t, n_row), c, z), device_id_type=MESH)

    @pl.when(has_up)
    def _():
        pl.semaphore_signal(barrier, inc=1, device_id=above, device_id_type=MESH)

    @pl.when(has_down)
    def _():
        pl.semaphore_signal(barrier, inc=1, device_id=below, device_id_type=MESH)

    pl.semaphore_wait(barrier, n_row - 1 + has_up.astype(jnp.int32) + has_down.astype(jnp.int32))

    def part(ref, block, q):
        if ref is own_ref:
            return ref.at[block, pl.ds(pl.multiple_of(q * rows, 8), rows)]
        return ref.at[pl.ds(pl.multiple_of(block * rows_tile + q * rows, 8), rows)]

    def along_row(t, q, outward):
        peer = lax.rem(r + t, n_row)
        return pltpu.make_async_remote_copy(
            src_ref=part(own_ref, peer, q),
            dst_ref=part(out_ref, z * n_row + r if outward else z * n_row + lax.rem(r - t + n_row, n_row), q),
            send_sem=y_send.at[t * chunks + q],
            recv_sem=y_recv.at[t * chunks + q],
            device_id=(peer, c, z),
            device_id_type=MESH,
        )

    def along_rep(source, block, q, sems, target):
        return pltpu.make_async_remote_copy(
            src_ref=part(*source, q),
            dst_ref=part(out_ref, block, q),
            send_sem=sems.at[block * chunks + q],
            recv_sem=z_recv.at[block * chunks + q],
            device_id=target,
            device_id_type=MESH,
        )

    def forward(source, block, q):
        @pl.when(has_up)
        def _():
            along_rep(source, block, q, up_send, above).start()

        @pl.when(has_down)
        def _():
            along_rep(source, block, q, down_send, below).start()

    level_rows = n_row * rows_tile
    by_level = level_rows % LANES == 0
    cols = out_ref.shape[1]
    tile = 256 if cols % 256 == 0 else LANES

    def multiply(first, depth, fresh):
        within = pl.ds(first, depth)

        @pl.loop(0, cols // tile)
        def _(n):
            at = pl.ds(pl.multiple_of(n * tile, tile), tile)
            term = jnp.dot(
                hidden_ref[:, within], out_ref[within, at], preferred_element_type=jnp.float32
            )
            projected_ref[:, at] = term if fresh else projected_ref[:, at] + term

    def add_level(level, fresh=False):
        if by_level:
            multiply(pl.multiple_of(level * level_rows, LANES), level_rows, fresh)

    mine = z * n_row + r

    @pl.loop(0, chunks)
    def _(q):
        forward((own_ref, r), mine, q)
        for t in range(1, n_row):
            along_row(t, q, True).start()

    step = 16 if rows_tile % 16 == 0 else 8

    @pl.loop(0, rows_tile // step)
    def _(i):
        at = pl.ds(pl.multiple_of(i * step, step), step)
        to = pl.ds(pl.multiple_of(mine * rows_tile + i * step, step), step)
        out_ref[to, :] = own_ref[r, at, :]

    for t in range(1, n_row):

        @pl.loop(0, chunks)
        def _(q):
            along_row(t, q, False).wait_recv()
            block = z * n_row + lax.rem(r - t + n_row, n_row)
            forward((out_ref, block), block, q)

    def arrived(level, i, sems, target, onward):
        t, q = i // chunks, lax.rem(i, chunks)
        block = level * n_row + lax.rem(r - t + n_row, n_row)
        copy = along_rep((out_ref, block), block, q, sems, target)
        copy.wait_recv()

        @pl.when(onward)
        def _():
            copy.start()

    add_level(z, True)

    @pl.loop(1, n_rep)
    def _(d):
        @pl.loop(0, per_level)
        def _(i):
            @pl.when(z - d >= 0)
            def _():
                arrived(z - d, i, up_send, above, has_up)

            @pl.when(z + d < n_rep)
            def _():
                arrived(z + d, i, down_send, below, has_down)

        @pl.when(z - d >= 0)
        def _():
            add_level(z - d)

        @pl.when(z + d < n_rep)
        def _():
            add_level(z + d)

    if not by_level:
        multiply(0, out_ref.shape[0], True)

    @pl.loop(0, chunks)
    def _(q):
        for t in range(1, n_row):
            along_row(t, q, True).wait_send()

    def drain(first, last, sems, target):
        @pl.loop(first * per_level, last * per_level)
        def _(i):
            block, q = i // chunks, lax.rem(i, chunks)
            along_rep((out_ref, block), block, q, sems, target).wait_send()

    @pl.when(has_up)
    def _():
        drain(0, z + 1, up_send, above)

    @pl.when(has_down)
    def _():
        drain(z, n_rep, down_send, below)


def gathered(own, hidden):
    n_row, n_rep = lax.axis_size("row"), lax.axis_size("rep")
    _, rows_tile, piece_cols = own.shape
    chunks = 4 if rows_tile % 64 == 0 else 1
    every = n_rep * n_row * chunks
    dma = pltpu.SemaphoreType.DMA
    return pl.pallas_call(
        functools.partial(gather_kernel, n_row, n_rep, chunks),
        out_shape=(
            pltpu.VMEM((n_rep * n_row * rows_tile, piece_cols), own.dtype),
            pltpu.VMEM((hidden.shape[0], piece_cols), jnp.float32),
        ),
        in_specs=[pl.BlockSpec(memory_space=pltpu.VMEM)] * 2,
        out_specs=(pl.BlockSpec(memory_space=pltpu.VMEM),) * 2,
        scratch_shapes=[
            dma((n_row * chunks,)),
            dma((n_row * chunks,)),
            dma((every,)),
            dma((every,)),
            dma((every,)),
        ],
        compiler_params=pltpu.CompilerParams(
            collective_id=0, has_side_effects=True, vmem_limit_bytes=VMEM_LIMIT
        ),
    )(pltpu.with_memory_space_constraint(own, pltpu.VMEM), hidden)


def store_kernel(landed_ref, served_ref, sem):
    parts = sem.shape[0]
    rows = served_ref.shape[0] // parts
    copies = [
        pltpu.make_async_copy(
            landed_ref.at[pl.ds(i * rows, rows)], served_ref.at[pl.ds(i * rows, rows)], sem.at[i]
        )
        for i in range(parts)
    ]
    for copy in copies:
        copy.start()
    for copy in copies:
        copy.wait()


def stored(landed):
    return pl.pallas_call(
        store_kernel,
        out_shape=jax.ShapeDtypeStruct(landed.shape, landed.dtype),
        in_specs=[pl.BlockSpec(memory_space=pl.ANY)],
        out_specs=pl.BlockSpec(memory_space=pl.ANY),
        scratch_shapes=[pltpu.SemaphoreType.DMA((8,))],
        compiler_params=pltpu.CompilerParams(vmem_limit_bytes=1024 * 1024),
    )(landed)


def shards(hidden, train_weight, shard_order):
    landed, projected = gathered(ordered_pieces(train_weight, shard_order), hidden)
    return stored(landed), projected


def solution(mesh):
    placed = (P("rep", None), P(("rep", "row"), "col"), P())
    return jax.shard_map(
        shards,
        mesh=mesh,
        in_specs=placed,
        out_specs=(P(None, ("col", "row")), P("rep", ("col", "row"))),
        check_vma=False,
    )
```

profile of v0, /device:TPU:0, one launch (start us, length us, event | category | flops | bytes accessed | tf_op | source)
XLA Modules:
  0.0 496.9 jit_solution(6754760068358220525)
XLA Ops:
  0.6 0.8 copy.5.order_ref
  1.4 0.0 copy-start
  1.4 3.9 shard_map.50.own_ref
  5.3 0.0 copy-done
  5.3 480.7 %shard_map.51 = (bf16[7168,2048]{1,0:T(8,128)(2,1)S(1)}, f32[128,2048]{1,0:T(8,128)S(1)}) custom-call(bf16[2,896,2048]{2,1,0:T(8,128)(2,1)S(1)} %shard_map.50.own_ref, bf16[128,7168]{1,0:T(8,128)(2,1)S(1)} %copy-done), custom_call_target="tpu_custom_call" | custom-call | tf_op jit(solution)/shard_map/pallas_call | solution.py:228
  486.1 9.8 %shard_map.52 = bf16[7168,2048]{1,0:T(8,128)(2,1)} custom-call(bf16[7168,2048]{1,0:T(8,128)(2,1)S(1)} %get-tuple-element.4.landed_ref), custom_call_target="tpu_custom_call" | custom-call | tf_op jit(solution)/shard_map/pallas_call | solution.py:265
  495.9 1.0 copy.7
Async XLA Ops:
  1.4 3.9 copy-start
where the time goes:
time: 497 us
  Pallas kernels  494 us (99%)
    pallas_call x1, Pallas kernels, gathered(): pl.pallas_call(functools.partial(gather_kernel, n_row, n_rep, chunks), ou...  481 us

commit v1 on v0

v1 whole, which is shorter than its diff:
```python
import functools

import jax
import jax.numpy as jnp
from jax import lax
from jax.experimental import pallas as pl
from jax.experimental.pallas import tpu as pltpu
from jax.sharding import PartitionSpec as P

MESH = pl.DeviceIdType.MESH
LANES = 128
MIB = 1024 * 1024
LATE_CHUNKS = (0, 0)


def ordered_pieces(tile, shard_order):
    _, sub_count, row_count = shard_order.shape
    rows_tile, cols_tile = tile.shape
    piece_cols = cols_tile // row_count
    sub_cols = piece_cols // sub_count
    my_order = lax.dynamic_index_in_dim(shard_order, lax.axis_index("col"), 0, keepdims=False)
    blocks = tile.reshape(rows_tile, row_count, sub_count, sub_cols)
    pieces = []
    for s in range(row_count):
        piece = blocks[:, 0]
        for j in range(1, row_count):
            piece = jnp.where((my_order[:, s] == j)[None, :, None], blocks[:, j], piece)
        pieces.append(piece.reshape(rows_tile, piece_cols))
    return jnp.concatenate(pieces, axis=1)


def late_start(chunks, late):
    return chunks - jnp.where(lax.rem(lax.axis_index("col"), 2) == 0, late[0], late[1])


def row_tiles(cols):
    return 256 if cols % 256 == 0 else LANES


def handoff_kernel(
    n_row, n_rep, chunks, late, reorder,
    order_ref, tile_ref, hidden_hbm, full_ref, projected_ref,
    raw_ref, away_ref, hidden_ref, raw_sem, hidden_sem, y_send, y_recv, z_recv, up_send, down_send,
):
    r, c, z = lax.axis_index("row"), lax.axis_index("col"), lax.axis_index("rep")
    rows_tile, cols_tile = tile_ref.shape
    cols = cols_tile // n_row
    rows = rows_tile // chunks
    has_up, has_down = z < n_rep - 1, z > 0
    above = (r, c, jnp.minimum(z + 1, n_rep - 1))
    below = (r, c, jnp.maximum(z - 1, 0))
    per_level = n_row * chunks
    mine = z * n_row + r
    kept = (n_row - 1) * chunks + late_start(chunks, late)

    barrier = pltpu.get_barrier_semaphore()
    for t in range(1, n_row):
        pl.semaphore_signal(barrier, inc=1, device_id=(lax.rem(r + t, n_row), c, z), device_id_type=MESH)

    @pl.when(has_up)
    def _():
        pl.semaphore_signal(barrier, inc=1, device_id=above, device_id_type=MESH)

    @pl.when(has_down)
    def _():
        pl.semaphore_signal(barrier, inc=1, device_id=below, device_id_type=MESH)

    def chunk_of(ref, block, q):
        return ref.at[pl.ds(pl.multiple_of(block * rows_tile + q * rows, 8), rows)]

    def staged(q):
        return pltpu.make_async_copy(chunk_of(tile_ref, 0, q), chunk_of(raw_ref, 0, q), raw_sem.at[q])

    @pl.loop(0, chunks)
    def _(q):
        staged(q).start()

    hidden_copy = pltpu.make_async_copy(hidden_hbm, hidden_ref, hidden_sem)
    hidden_copy.start()

    sub_count = order_ref.shape[2]
    sub_cols = cols // sub_count
    step = 16 if rows % 16 == 0 else 8

    def arrange(q):
        staged(q).wait()

        @pl.loop(0, rows // step)
        def _(i):
            at = pl.ds(pl.multiple_of(q * rows + i * step, step), step)
            to = pl.ds(pl.multiple_of(mine * rows_tile + q * rows + i * step, step), step)

            def place(t, span, piece):
                if t == 0:
                    full_ref[to, span] = piece
                else:
                    away_ref[t - 1, at, span] = piece

            if reorder:
                for k in range(sub_count):
                    blocks = [raw_ref[at, pl.ds(j * cols + k * sub_cols, sub_cols)] for j in range(n_row)]
                    for t in range(n_row):
                        s = lax.rem(r + t, n_row)
                        piece = blocks[0]
                        for j in range(1, n_row):
                            piece = jnp.where(order_ref[c, s, k] == j, blocks[j], piece)
                        place(t, pl.ds(k * sub_cols, sub_cols), piece)
            else:
                for t in range(n_row):
                    s = lax.rem(r + t, n_row)
                    place(t, pl.ds(0, cols), raw_ref[at, pl.ds(pl.multiple_of(s * cols, LANES), cols)])

    def along_row(t, q, outward):
        peer = lax.rem(r + t, n_row)
        source = lax.rem(r - t + n_row, n_row)
        return pltpu.make_async_remote_copy(
            src_ref=chunk_of(away_ref.at[t - 1], 0, q),
            dst_ref=chunk_of(full_ref, z * n_row + (r if outward else source), q),
            send_sem=y_send.at[t * chunks + q],
            recv_sem=y_recv.at[t * chunks + q],
            device_id=(peer, c, z),
            device_id_type=MESH,
        )

    def along_rep(block, q, sems, target):
        return pltpu.make_async_remote_copy(
            src_ref=chunk_of(full_ref, block, q),
            dst_ref=chunk_of(full_ref, block, q),
            send_sem=sems.at[block * chunks + q],
            recv_sem=z_recv.at[block * chunks + q],
            device_id=target,
            device_id_type=MESH,
        )

    def forward(block, q):
        @pl.when(has_up)
        def _():
            along_rep(block, q, up_send, above).start()

        @pl.when(has_down)
        def _():
            along_rep(block, q, down_send, below).start()

    by_chunk = rows % LANES == 0
    tile = row_tiles(cols)

    def multiply(first, depth, fresh):
        within = pl.ds(first, depth)

        @pl.loop(0, cols // tile)
        def _(n):
            at = pl.ds(pl.multiple_of(n * tile, tile), tile)
            term = jnp.dot(hidden_ref[:, within], full_ref[within, at], preferred_element_type=jnp.float32)
            projected_ref[:, at] = term if fresh else projected_ref[:, at] + term

    def consume(block, q):
        if by_chunk:
            multiply(pl.multiple_of(block * rows_tile + q * rows, LANES), rows, False)

    def send_own(q):
        forward(mine, q)
        for t in range(1, n_row):
            along_row(t, q, True).start()

    arrange(0)
    pl.semaphore_wait(barrier, n_row - 1 + has_up.astype(jnp.int32) + has_down.astype(jnp.int32))

    @pl.loop(1, chunks)
    def _(q):
        arrange(q)
        send_own(q - 1)

    send_own(chunks - 1)

    if by_chunk:
        projected_ref[...] = jnp.zeros_like(projected_ref)
    hidden_copy.wait()

    @pl.loop(0, chunks)
    def _(q):
        consume(mine, q)

    for t in range(1, n_row):

        @pl.loop(0, chunks)
        def _(q):
            along_row(t, q, False).wait_recv()
            block = z * n_row + lax.rem(r - t + n_row, n_row)
            forward(block, q)
            consume(block, q)

    def block_of(level, i):
        return level * n_row + lax.rem(r - i // chunks + n_row, n_row), lax.rem(i, chunks)

    def arrived(level, i, sems, target, onward):
        block, q = block_of(level, i)
        copy = along_rep(block, q, sems, target)
        copy.wait_recv()

        @pl.when(onward)
        def _():
            copy.start()

        consume(block, q)

    @pl.loop(1, n_rep)
    def _(d):
        @pl.loop(0, per_level)
        def _(i):
            @pl.when(z - d >= 0)
            def _():
                @pl.when((d < n_rep - 1) | (i < kept))
                def _():
                    arrived(z - d, i, up_send, above, has_up & ((z - d > 0) | (z + 1 < n_rep - 1) | (i < kept)))

            @pl.when(z + d < n_rep)
            def _():
                @pl.when((d < n_rep - 1) | (i < kept))
                def _():
                    arrived(z + d, i, down_send, below, has_down & ((z + d < n_rep - 1) | (z > 1) | (i < kept)))

    if not by_chunk:
        multiply(0, full_ref.shape[0], True)

    @pl.loop(0, chunks)
    def _(q):
        for t in range(1, n_row):
            along_row(t, q, True).wait_send()

    def drain(level, sent, sems, target):
        @pl.loop(0, sent)
        def _(i):
            block, q = block_of(level, i)
            along_rep(block, q, sems, target).wait_send()

    @pl.when(has_up)
    def _():
        @pl.loop(0, z + 1)
        def _(level):
            drain(level, jnp.where((level == 0) & (z + 1 == n_rep - 1), kept, per_level), up_send, above)

    @pl.when(has_down)
    def _():
        @pl.loop(z, n_rep)
        def _(level):
            drain(level, jnp.where((level == n_rep - 1) & (z == 1), kept, per_level), down_send, below)


def vmem():
    return pl.BlockSpec(memory_space=pltpu.VMEM)


def in_hbm(x):
    return pltpu.with_memory_space_constraint(x, pltpu.HBM)


def hbm():
    return pl.BlockSpec(memory_space=pltpu.HBM)


def handed_off(hidden, tile, shard_order, chunks, late, reorder):
    n_row, n_rep = lax.axis_size("row"), lax.axis_size("rep")
    rows_tile, cols_tile = tile.shape
    cols = cols_tile // n_row
    every = n_rep * n_row * chunks
    dma = pltpu.SemaphoreType.DMA
    height = n_rep * n_row * rows_tile
    return pl.pallas_call(
        functools.partial(handoff_kernel, n_row, n_rep, chunks, late, reorder),
        out_shape=(
            pltpu.VMEM((height, cols), tile.dtype),
            pltpu.VMEM((hidden.shape[0], cols), jnp.float32),
        ),
        in_specs=[pl.BlockSpec(memory_space=pltpu.SMEM), hbm(), hbm()],
        out_specs=(vmem(), vmem()),
        scratch_shapes=[
            pltpu.VMEM((rows_tile, cols_tile), tile.dtype),
            pltpu.VMEM((n_row - 1, rows_tile, cols), tile.dtype),
            pltpu.VMEM(hidden.shape, hidden.dtype),
            dma((chunks,)),
            dma,
            dma((n_row * chunks,)),
            dma((n_row * chunks,)),
            dma((every,)),
            dma((every,)),
            dma((every,)),
        ],
        compiler_params=pltpu.CompilerParams(
            collective_id=0, has_side_effects=True, vmem_limit_bytes=14 * MIB
        ),
    )(jnp.swapaxes(shard_order, 1, 2), in_hbm(tile), in_hbm(hidden))


def store_kernel(landed_ref, served_ref, sem):
    parts = sem.shape[0] - 1
    rows = served_ref.shape[0] // parts
    copies = [
        pltpu.make_async_copy(
            landed_ref.at[pl.ds(i * rows, rows)], served_ref.at[pl.ds(i * rows, rows)], sem.at[i]
        )
        for i in range(parts)
    ]
    for copy in copies:
        copy.start()
    for copy in copies:
        copy.wait()


def stored(landed, summed):
    return pl.pallas_call(
        store_kernel,
        out_shape=jax.ShapeDtypeStruct(landed.shape, landed.dtype),
        in_specs=[pl.BlockSpec(memory_space=pl.ANY)],
        out_specs=pl.BlockSpec(memory_space=pl.ANY),
        scratch_shapes=[pltpu.SemaphoreType.DMA((9,))],
        compiler_params=pltpu.CompilerParams(vmem_limit_bytes=MIB),
    )(landed), summed


def shards(hidden, train_weight, shard_order):
    _, sub_count, n_row = shard_order.shape
    rows_tile, cols_tile = train_weight.shape
    chunks = rows_tile // LANES if rows_tile % LANES == 0 else 1
    late = LATE_CHUNKS if chunks > max(LATE_CHUNKS) else (0, 0)
    reorder = (cols_tile // (n_row * sub_count)) % LANES == 0
    tile = train_weight if reorder else ordered_pieces(train_weight, shard_order)
    landed, summed = handed_off(hidden, tile, shard_order, chunks, late, reorder)
    return stored(landed, summed)


def solution(mesh):
    placed = (P("rep", None), P(("rep", "row"), "col"), P())
    return jax.shard_map(
        shards,
        mesh=mesh,
        in_specs=placed,
        out_specs=(P(None, ("col", "row")), P("rep", ("col", "row"))),
        check_vma=False,
    )
```

time: 497 us -> 494 us (level)
    pallas_call x2 -> x1, Pallas kernels: 485 us -> 481 us  [handed_off(): pl.pallas_call(functools.partial(handoff_kernel, n_row, n_rep, chunks, la...]
where the time goes in v1:
time: 494 us
  Pallas kernels  491 us (99%)
    pallas_call x1, Pallas kernels, handed_off(): pl.pallas_call(functools.partial(handoff_kernel, n_row, n_rep, chunks, la...  481 us

profile of v1, /device:TPU:0, one launch (start us, length us, event | category | flops | bytes accessed | tf_op | source)
XLA Modules:
  0.0 493.5 jit_solution(13563423285967656565)
XLA Ops:
  0.6 0.0 copy-start
  0.6 0.7 copy-done
  1.3 481.4 %shard_map.50 = (bf16[7168,2048]{1,0:T(8,128)(2,1)S(1)}, f32[128,2048]{1,0:T(8,128)S(1)}) custom-call(s32[4,2,4]{2,1,0:T(2,128)S(1)} %bitcast.1, bf16[896,4096]{1,0:T(8,128)(2,1)} %tile_ref.1, bf16[128,7168]{1,0:T(8,128)(2,1)} %hidden_hbm.1), custom_call_target="tpu_custom_call" | custom-call | tf_op jit(solution)/shard_map/pallas_call | solution.py:268
  482.7 9.9 %shard_map.51 = bf16[7168,2048]{1,0:T(8,128)(2,1)} custom-call(bf16[7168,2048]{1,0:T(8,128)(2,1)S(1)} %get-tuple-element.4.landed_ref), custom_call_target="tpu_custom_call" | custom-call | tf_op jit(solution)/shard_map/pallas_call | solution.py:310
  492.6 1.0 copy.6
Async XLA Ops:
  0.6 0.7 copy-start

commit v2 on v1

--- a/solution.py
+++ b/solution.py
@@ -10,7 +10,7 @@
 MESH = pl.DeviceIdType.MESH
 LANES = 128
 MIB = 1024 * 1024
-LATE_CHUNKS = (0, 0)
+LATE_CHUNKS = (6, 3)
 
 
 def ordered_pieces(tile, shard_order):
@@ -39,7 +39,7 @@
 
 def handoff_kernel(
     n_row, n_rep, chunks, late, reorder,
-    order_ref, tile_ref, hidden_hbm, full_ref, projected_ref,
+    order_ref, tile_ref, hidden_hbm, full_ref, projected_ref, keep_ref,
     raw_ref, away_ref, hidden_ref, raw_sem, hidden_sem, y_send, y_recv, z_recv, up_send, down_send,
 ):
     r, c, z = lax.axis_index("row"), lax.axis_index("col"), lax.axis_index("rep")
@@ -192,16 +192,25 @@
     def block_of(level, i):
         return level * n_row + lax.rem(r - i // chunks + n_row, n_row), lax.rem(i, chunks)
 
-    def arrived(level, i, sems, target, onward):
+    def arrived(d, level, i, sems, target, onward):
         block, q = block_of(level, i)
         copy = along_rep(block, q, sems, target)
         copy.wait_recv()
-
-        @pl.when(onward)
+        deferred = (d == n_rep - 2) & (i >= kept)
+
+        @pl.when(onward & jnp.logical_not(deferred))
         def _():
             copy.start()
 
         consume(block, q)
+        if max(late):
+
+            @pl.when(onward & deferred)
+            def _():
+                slot = q - (chunks - max(late))
+                keep_ref[pl.ds(pl.multiple_of(slot * rows, LANES), rows), :] = full_ref[
+                    pl.ds(pl.multiple_of(block * rows_tile + q * rows, LANES), rows), :
+                ]
 
     @pl.loop(1, n_rep)
     def _(d):
@@ -211,13 +220,13 @@
             def _():
                 @pl.when((d < n_rep - 1) | (i < kept))
                 def _():
-                    arrived(z - d, i, up_send, above, has_up & ((z - d > 0) | (z + 1 < n_rep - 1) | (i < kept)))
+                    arrived(d, z - d, i, up_send, above, has_up)
 
             @pl.when(z + d < n_rep)
             def _():
                 @pl.when((d < n_rep - 1) | (i < kept))
                 def _():
-                    arrived(z + d, i, down_send, below, has_down & ((z + d < n_rep - 1) | (z > 1) | (i < kept)))
+                    arrived(d, z + d, i, down_send, below, has_down)
 
     if not by_chunk:
         multiply(0, full_ref.shape[0], True)
@@ -270,9 +279,10 @@
         out_shape=(
             pltpu.VMEM((height, cols), tile.dtype),
             pltpu.VMEM((hidden.shape[0], cols), jnp.float32),
+            pltpu.VMEM((max(8, max(late) * (rows_tile // chunks)), cols), tile.dtype),
         ),
         in_specs=[pl.BlockSpec(memory_space=pltpu.SMEM), hbm(), hbm()],
-        out_specs=(vmem(), vmem()),
+        out_specs=(vmem(),) * 3,
         scratch_shapes=[
             pltpu.VMEM((rows_tile, cols_tile), tile.dtype),
             pltpu.VMEM((n_row - 1, rows_tile, cols), tile.dtype),
@@ -292,7 +302,7 @@
 
 
 def store_kernel(landed_ref, served_ref, sem):
-    parts = sem.shape[0] - 1
+    parts = sem.shape[0]
     rows = served_ref.shape[0] // parts
     copies = [
         pltpu.make_async_copy(
@@ -306,26 +316,200 @@
         copy.wait()
 
 
-def stored(landed, summed):
+def stored(landed):
     return pl.pallas_call(
         store_kernel,
         out_shape=jax.ShapeDtypeStruct(landed.shape, landed.dtype),
         in_specs=[pl.BlockSpec(memory_space=pl.ANY)],
         out_specs=pl.BlockSpec(memory_space=pl.ANY),
-        scratch_shapes=[pltpu.SemaphoreType.DMA((9,))],
+        scratch_shapes=[pltpu.SemaphoreType.DMA((8,))],
         compiler_params=pltpu.CompilerParams(vmem_limit_bytes=MIB),
-    )(landed), summed
+    )(landed)
+
+
+def late_kernel(
+    n_row, n_rep, chunks, late,
+    keep_ref, partial_ref, hidden_hbm, _, late_ref, summed_ref,
+    hidden_ref, hidden_sem, send_sem, recv_sem,
+):
+    r, c, z = lax.axis_index("row"), lax.axis_index("col"), lax.axis_index("rep")
+    slots = max(late)
+    rows, cols = late_ref.shape[0] // slots, late_ref.shape[1]
+    first = late_start(chunks, late)
+    other = lax.rem(r + 1, n_row)
+    lowest, highest = other, (n_rep - 1) * n_row + other
+    gives_up, gives_down = z == n_rep - 2, z == 1
+    takes_below, takes_above = z == n_rep - 1, z == 0
+    above = (r, c, jnp.minimum(z + 1, n_rep - 1))
+    below = (r, c, jnp.maximum(z - 1, 0))
+
+    barrier = pltpu.get_barrier_semaphore()
+
+    @pl.when(gives_up | takes_above)
+    def _():
+        pl.semaphore_signal(barrier, inc=1, device_id=above, device_id_type=MESH)
+
+    @pl.when(gives_down | takes_below)
+    def _():
+        pl.semaphore_signal(barrier, inc=1, device_id=below, device_id_type=MESH)
+
+    pl.semaphore_wait(barrier, (gives_up | takes_above).astype(jnp.int32) + (gives_down | takes_below).astype(jnp.int32))
+
+    def moved(q, target):
+        slot = q - (chunks - slots)
+        return pltpu.make_async_remote_copy(
+            src_ref=keep_ref.at[pl.ds(pl.multiple_of(slot * rows, LANES), rows)],
+            dst_ref=late_ref.at[pl.ds(pl.multiple_of(slot * rows, LANES), rows)],
+            send_sem=send_sem.at[slot],
+            recv_sem=recv_sem.at[slot],
+            device_id=target,
+            device_id_type=MESH,
+        )
+
+    @pl.when(gives_up)
+    def _():
+        @pl.loop(first, chunks)
+        def _(q):
+            moved(q, above).start()
+
+    @pl.when(gives_down)
+    def _():
+        @pl.loop(first, chunks)
+        def _(q):
+            moved(q, below).start()
+
+    summed_ref[...] = partial_ref[...]
+    tile = row_tiles(cols)
+
+    def take(block, target):
+        hidden_copy = pltpu.make_async_copy(
+            hidden_hbm.at[:, pl.ds(pl.multiple_of((block * chunks + chunks - slots) * rows, LANES), slots * rows)],
+            hidden_ref,
+            hidden_sem,
+        )
+        hidden_copy.start()
+        hidden_copy.wait()
+
+        @pl.loop(first, chunks)
+        def _(q):
+            moved(q, target).wait_recv()
+            within = pl.ds(pl.multiple_of((q - (chunks - slots)) * rows, LANES), rows)
+            for n in range(cols // tile):
+                at = pl.ds(n * tile, tile)
+                summed_ref[:, at] += jnp.dot(
+                    hidden_ref[:, within], late_ref[within, at], preferred_element_type=jnp.float32
+                )
+
+    @pl.when(takes_below)
+    def _():
+        take(lowest, below)
+
+    @pl.when(takes_above)
+    def _():
+        take(highest, above)
+
+    @pl.when(gives_up)
+    def _():
+        @pl.loop(first, chunks)
+        def _(q):
+            moved(q, above).wait_send()
+
+    @pl.when(gives_down)
+    def _():
+        @pl.loop(first, chunks)
+        def _(q):
+            moved(q, below).wait_send()
+
+
+def late_handoff(keep, partial, hidden, token, chunks, late):
+    n_row, n_rep = lax.axis_size("row"), lax.axis_size("rep")
+    slots = max(late)
+    rows = keep.shape[0] // slots
+    dma = pltpu.SemaphoreType.DMA
+    return pl.pallas_call(
+        functools.partial(late_kernel, n_row, n_rep, chunks, late),
+        out_shape=(
+            pltpu.VMEM(keep.shape, keep.dtype),
+            pltpu.VMEM(partial.shape, partial.dtype),
+        ),
+        in_specs=[vmem(), vmem(), hbm(), hbm()],
+        out_specs=(vmem(), vmem()),
+        scratch_shapes=[
+            pltpu.VMEM((hidden.shape[0], slots * rows), hidden.dtype),
+            dma,
+            dma((slots,)),
+            dma((slots,)),
+        ],
+        cost_estimate=pl.CostEstimate(flops=10**11, bytes_accessed=10**6, transcendentals=0),
+        compiler_params=pltpu.CompilerParams(
+            collective_id=1, has_side_effects=True, vmem_limit_bytes=2 * MIB
+        ),
+    )(keep, partial, in_hbm(hidden), in_hbm(token))
+
+
+def finish_kernel(n_row, n_rep, chunks, late, early_ref, late_ref, summed_ref, served_ref, projected_ref, sem, projected_sem):
+    r, z = lax.axis_index("row"), lax.axis_index("rep")
+    rows_tile = served_ref.shape[0] // (n_row * n_rep)
+    rows = rows_tile // chunks
+    slots = late_ref.shape[0] // rows
+    first = late_start(chunks, late)
+    block = jnp.where(z == 0, n_rep - 1, 0) * n_row + lax.rem(r + 1, n_row)
+    takes = (z == 0) | (z == n_rep - 1)
+
+    def stored(q):
+        slot = q - (chunks - slots)
+        return pltpu.make_async_copy(
+            late_ref.at[pl.ds(pl.multiple_of(slot * rows, LANES), rows)],
+            served_ref.at[pl.ds(pl.multiple_of(block * rows_tile + q * rows, LANES), rows)],
+            sem.at[slot],
+        )
+
+    projected_copy = pltpu.make_async_copy(summed_ref, projected_ref, projected_sem)
+    projected_copy.start()
+
+    @pl.when(takes)
+    def _():
+        @pl.loop(first, chunks)
+        def _(q):
+            stored(q).start()
+
+        @pl.loop(first, chunks)
+        def _(q):
+            stored(q).wait()
+
+    projected_copy.wait()
+
+
+def finished(early, landed, summed, chunks, late):
+    n_row, n_rep = lax.axis_size("row"), lax.axis_size("rep")
+    dma = pltpu.SemaphoreType.DMA
+    return pl.pallas_call(
+        functools.partial(finish_kernel, n_row, n_rep, chunks, late),
+        out_shape=(
+            jax.ShapeDtypeStruct(early.shape, early.dtype),
+            jax.ShapeDtypeStruct(summed.shape, summed.dtype),
+        ),
+        in_specs=[pl.BlockSpec(memory_space=pl.ANY), vmem(), vmem()],
+        out_specs=(pl.BlockSpec(memory_space=pl.ANY),) * 2,
+        scratch_shapes=[dma((max(late),)), dma],
+        input_output_aliases={0: 0},
+        compiler_params=pltpu.CompilerParams(vmem_limit_bytes=MIB),
+    )(early, landed, summed)
 
 
 def shards(hidden, train_weight, shard_order):
     _, sub_count, n_row = shard_order.shape
     rows_tile, cols_tile = train_weight.shape
     chunks = rows_tile // LANES if rows_tile % LANES == 0 else 1
-    late = LATE_CHUNKS if chunks > max(LATE_CHUNKS) else (0, 0)
+    late = LATE_CHUNKS if chunks > max(LATE_CHUNKS) and lax.axis_size("rep") > 2 else (0, 0)
     reorder = (cols_tile // (n_row * sub_count)) % LANES == 0
     tile = train_weight if reorder else ordered_pieces(train_weight, shard_order)
-    landed, summed = handed_off(hidden, tile, shard_order, chunks, late, reorder)
-    return stored(landed, summed)
+    landed, summed, keep = handed_off(hidden, tile, shard_order, chunks, late, reorder)
+    served = stored(landed)
+    if max(late) == 0:
+        return served, summed
+    tail, total = late_handoff(keep, summed, hidden, served, chunks, late)
+    return finished(served, tail, total, chunks, late)
 
 
 def solution(mesh):

time: 494 us -> 483 us (0.978)
  Pallas kernels: 491 us -> 481 us
    pallas_call x1, Pallas kernels: 481 us -> 415 us  [handed_off(): pl.pallas_call(functools.partial(handoff_kernel, n_row, n_rep, chunks, la...]
    pallas_call x0 -> x2, Pallas kernels: none -> 56.6 us  [the longest x1 54.6 us: late_handoff(): pl.pallas_call(functools.partial(late_kernel, n_row, n_rep, chunks, late)...]
where the time goes in v2:
time: 483 us
  Pallas kernels  481 us (100%)
    pallas_call x1, Pallas kernels, handed_off(): pl.pallas_call(functools.partial(handoff_kernel, n_row, n_rep, chunks, la...  415 us
    pallas_call x1, Pallas kernels, late_handoff(): pl.pallas_call(functools.partial(late_kernel, n_row, n_rep, chunks, late)...  54.6 us
    pallas_call x1, Pallas kernels, stored(): pl.pallas_call(store_kernel, out_shape=jax.ShapeDtypeStruct(landed.shape,...  9.84 us

profile of v2, /device:TPU:0, one launch (start us, length us, event | category | flops | bytes accessed | tf_op | source)
XLA Modules:
  0.0 482.8 jit_solution(2886077205694733025)
XLA Ops:
  0.6 0.0 copy-start
  0.6 0.7 copy-done
  1.3 415.0 %shard_map.50 = (bf16[7168,2048]{1,0:T(8,128)(2,1)S(1)}, f32[128,2048]{1,0:T(8,128)S(1)}, bf16[768,2048]{1,0:T(8,128)(2,1)S(1)}) custom-call(s32[4,2,4]{2,1,0:T(2,128)S(1)} %bitcast.1, bf16[896,4096]{1,0:T(8,128)(2,1)} %tile_ref.1, bf16[128,7168]{1,0:T(8,128)(2,1)} %hidden_hbm.3), custom_call_target="tpu_custom_call" | custom-call | tf_op jit(solution)/shard_map/pallas_call | solution.py:277
  416.3 9.8 %shard_map.51._.early_ref = bf16[7168,2048]{1,0:T(8,128)(2,1)} custom-call(bf16[7168,2048]{1,0:T(8,128)(2,1)S(1)} %get-tuple-element.7.landed_ref), custom_call_target="tpu_custom_call" | custom-call | tf_op jit(solution)/shard_map/pallas_call | solution.py:320
  426.2 54.6 %shard_map.52 = (bf16[768,2048]{1,0:T(8,128)(2,1)S(1)}, f32[128,2048]{1,0:T(8,128)S(1)}) custom-call(bf16[768,2048]{1,0:T(8,128)(2,1)S(1)} %get-tuple-element.8.keep_ref, f32[128,2048]{1,0:T(8,128)S(1)} %get-tuple-element.9.partial_ref, bf16[128,7168]{1,0:T(8,128)(2,1)} %hidden_hbm.3, bf16[7168,2048]{1,0:T(8,128)(2,1)} %shard_map.51._.early_ref), custom_call_target="tpu_custom_call" | custom-call | flops 99999997952 | bytes 1000000 | tf_op jit(solution)/shard_map/pallas_call | solution.py:429
  480.8 2.1 shard_map.53
Async XLA Ops:
  0.6 0.7 copy-start

commit v3 on v2

--- a/solution.py
+++ b/solution.py
@@ -10,7 +10,7 @@
 MESH = pl.DeviceIdType.MESH
 LANES = 128
 MIB = 1024 * 1024
-LATE_CHUNKS = (6, 3)
+LATE_CHUNKS = (5, 1)
 
 
 def ordered_pieces(tile, shard_order):
@@ -39,8 +39,8 @@
 
 def handoff_kernel(
     n_row, n_rep, chunks, late, reorder,
-    order_ref, tile_ref, hidden_hbm, full_ref, projected_ref, keep_ref,
-    raw_ref, away_ref, hidden_ref, raw_sem, hidden_sem, y_send, y_recv, z_recv, up_send, down_send,
+    order_hbm, tile_ref, hidden_hbm, full_ref, projected_ref, keep_ref,
+    order_ref, raw_ref, away_ref, hidden_ref, order_sem, raw_sem, hidden_sem, y_send, y_recv, z_recv, up_send, down_send,
 ):
     r, c, z = lax.axis_index("row"), lax.axis_index("col"), lax.axis_index("rep")
     rows_tile, cols_tile = tile_ref.shape
@@ -71,12 +71,10 @@
     def staged(q):
         return pltpu.make_async_copy(chunk_of(tile_ref, 0, q), chunk_of(raw_ref, 0, q), raw_sem.at[q])
 
-    @pl.loop(0, chunks)
-    def _(q):
-        staged(q).start()
-
+    order_copy = pltpu.make_async_copy(order_hbm, order_ref, order_sem)
     hidden_copy = pltpu.make_async_copy(hidden_hbm, hidden_ref, hidden_sem)
-    hidden_copy.start()
+    order_copy.start()
+    staged(0).start()
 
     sub_count = order_ref.shape[2]
     sub_cols = cols // sub_count
@@ -162,15 +160,27 @@
         for t in range(1, n_row):
             along_row(t, q, True).start()
 
+    order_copy.wait()
     arrange(0)
+
+    @pl.loop(1, chunks)
+    def _(q):
+        staged(q).start()
+
+    hidden_copy.start()
     pl.semaphore_wait(barrier, n_row - 1 + has_up.astype(jnp.int32) + has_down.astype(jnp.int32))
+    send_own(0)
 
     @pl.loop(1, chunks)
     def _(q):
         arrange(q)
-        send_own(q - 1)
-
-    send_own(chunks - 1)
+
+        @pl.when(q > 1)
+        def _():
+            send_own(q - 1)
+
+    if chunks > 1:
+        send_own(chunks - 1)
 
     if by_chunk:
         projected_ref[...] = jnp.zeros_like(projected_ref)
@@ -272,6 +282,7 @@
     rows_tile, cols_tile = tile.shape
     cols = cols_tile // n_row
     every = n_rep * n_row * chunks
+    order = jnp.swapaxes(shard_order, 1, 2)
     dma = pltpu.SemaphoreType.DMA
     height = n_rep * n_row * rows_tile
     return pl.pallas_call(
@@ -281,12 +292,14 @@
             pltpu.VMEM((hidden.shape[0], cols), jnp.float32),
             pltpu.VMEM((max(8, max(late) * (rows_tile // chunks)), cols), tile.dtype),
         ),
-        in_specs=[pl.BlockSpec(memory_space=pltpu.SMEM), hbm(), hbm()],
+        in_specs=[hbm(), hbm(), hbm()],
         out_specs=(vmem(),) * 3,
         scratch_shapes=[
+            pltpu.SMEM(order.shape, order.dtype),
             pltpu.VMEM((rows_tile, cols_tile), tile.dtype),
             pltpu.VMEM((n_row - 1, rows_tile, cols), tile.dtype),
             pltpu.VMEM(hidden.shape, hidden.dtype),
+            dma,
             dma((chunks,)),
             dma,
             dma((n_row * chunks,)),
@@ -298,7 +311,7 @@
         compiler_params=pltpu.CompilerParams(
             collective_id=0, has_side_effects=True, vmem_limit_bytes=14 * MIB
         ),
-    )(jnp.swapaxes(shard_order, 1, 2), in_hbm(tile), in_hbm(hidden))
+    )(in_hbm(order), in_hbm(tile), in_hbm(hidden))
 
 
 def store_kernel(landed_ref, served_ref, sem):

time: 483 us -> 480 us (level)
    pallas_call x1, Pallas kernels: 54.6 us -> 42.2 us  [late_handoff(): pl.pallas_call(functools.partial(late_kernel, n_row, n_rep, chunks, late)...]
    pallas_call x1, Pallas kernels: 415 us -> 425 us  [handed_off(): pl.pallas_call(functools.partial(handoff_kernel, n_row, n_rep, chunks, la...]
where the time goes in v3:
time: 480 us
  Pallas kernels  479 us (100%)
    pallas_call x1, Pallas kernels, handed_off(): pl.pallas_call(functools.partial(handoff_kernel, n_row, n_rep, chunks, la...  425 us
    pallas_call x1, Pallas kernels, late_handoff(): pl.pallas_call(functools.partial(late_kernel, n_row, n_rep, chunks, late)...  42.2 us
    pallas_call x1, Pallas kernels, stored(): pl.pallas_call(store_kernel, out_shape=jax.ShapeDtypeStruct(landed.shape,...  9.84 us

profile of v3, /device:TPU:0, one launch (start us, length us, event | category | flops | bytes accessed | tf_op | source)
XLA Modules:
  0.0 480.1 jit_solution(10643705334134765922)
XLA Ops:
  0.6 425.5 %shard_map.50 = (bf16[7168,2048]{1,0:T(8,128)(2,1)S(1)}, f32[128,2048]{1,0:T(8,128)S(1)}, bf16[640,2048]{1,0:T(8,128)(2,1)S(1)}) custom-call(s32[4,2,4]{2,1,0:T(2,128)} %bitcast.1, bf16[896,4096]{1,0:T(8,128)(2,1)} %tile_ref.1, bf16[128,7168]{1,0:T(8,128)(2,1)} %hidden_hbm.3), custom_call_target="tpu_custom_call" | custom-call | tf_op jit(solution)/shard_map/pallas_call | solution.py:288
  426.1 9.8 %shard_map.51._.early_ref = bf16[7168,2048]{1,0:T(8,128)(2,1)} custom-call(bf16[7168,2048]{1,0:T(8,128)(2,1)S(1)} %get-tuple-element.7.landed_ref), custom_call_target="tpu_custom_call" | custom-call | tf_op jit(solution)/shard_map/pallas_call | solution.py:333
  436.0 42.2 %shard_map.52 = (bf16[640,2048]{1,0:T(8,128)(2,1)S(1)}, f32[128,2048]{1,0:T(8,128)S(1)}) custom-call(bf16[640,2048]{1,0:T(8,128)(2,1)S(1)} %get-tuple-element.8.keep_ref, f32[128,2048]{1,0:T(8,128)S(1)} %get-tuple-element.9.partial_ref, bf16[128,7168]{1,0:T(8,128)(2,1)} %hidden_hbm.3, bf16[7168,2048]{1,0:T(8,128)(2,1)} %shard_map.51._.early_ref), custom_call_target="tpu_custom_call" | custom-call | flops 99999997952 | bytes 1000000 | tf_op jit(solution)/shard_map/pallas_call | solution.py:442
  478.2 1.9 shard_map.53

commit v4 on v3

--- a/solution.py
+++ b/solution.py
@@ -10,7 +10,7 @@
 MESH = pl.DeviceIdType.MESH
 LANES = 128
 MIB = 1024 * 1024
-LATE_CHUNKS = (5, 1)
+LATE_CHUNKS = (1, 6)
 
 
 def ordered_pieces(tile, shard_order):

time: 480 us -> 480 us (level)
    pallas_call x1, Pallas kernels: 425 us -> 454 us  [handed_off(): pl.pallas_call(functools.partial(handoff_kernel, n_row, n_rep, chunks, la...]
    pallas_call x1, Pallas kernels: 42.2 us -> 13.5 us  [late_handoff(): pl.pallas_call(functools.partial(late_kernel, n_row, n_rep, chunks, late)...]
where the time goes in v4:
time: 480 us; the launch traced here: 479 us
  Pallas kernels  479 us (100%)
    pallas_call x1, Pallas kernels, handed_off(): pl.pallas_call(functools.partial(handoff_kernel, n_row, n_rep, chunks, la...  454 us
    pallas_call x1, Pallas kernels, late_handoff(): pl.pallas_call(functools.partial(late_kernel, n_row, n_rep, chunks, late)...  13.5 us
    pallas_call x1, Pallas kernels, stored(): pl.pallas_call(store_kernel, out_shape=jax.ShapeDtypeStruct(landed.shape,...  9.84 us

profile of v4, /device:TPU:0, one launch (start us, length us, event | category | flops | bytes accessed | tf_op | source)
XLA Modules:
  0.0 479.4 jit_solution(5384390650577731185)
XLA Ops:
  0.6 454.1 %shard_map.50 = (bf16[7168,2048]{1,0:T(8,128)(2,1)S(1)}, f32[128,2048]{1,0:T(8,128)S(1)}, bf16[768,2048]{1,0:T(8,128)(2,1)S(1)}) custom-call(s32[4,2,4]{2,1,0:T(2,128)} %bitcast.1, bf16[896,4096]{1,0:T(8,128)(2,1)} %tile_ref.1, bf16[128,7168]{1,0:T(8,128)(2,1)} %hidden_hbm.3), custom_call_target="tpu_custom_call" | custom-call | tf_op jit(solution)/shard_map/pallas_call | solution.py:288
  454.8 9.8 %shard_map.51._.early_ref = bf16[7168,2048]{1,0:T(8,128)(2,1)} custom-call(bf16[7168,2048]{1,0:T(8,128)(2,1)S(1)} %get-tuple-element.7.landed_ref), custom_call_target="tpu_custom_call" | custom-call | tf_op jit(solution)/shard_map/pallas_call | solution.py:333
  464.6 13.5 %shard_map.52 = (bf16[768,2048]{1,0:T(8,128)(2,1)S(1)}, f32[128,2048]{1,0:T(8,128)S(1)}) custom-call(bf16[768,2048]{1,0:T(8,128)(2,1)S(1)} %get-tuple-element.8.keep_ref, f32[128,2048]{1,0:T(8,128)S(1)} %get-tuple-element.9.partial_ref, bf16[128,7168]{1,0:T(8,128)(2,1)} %hidden_hbm.3, bf16[7168,2048]{1,0:T(8,128)(2,1)} %shard_map.51._.early_ref), custom_call_target="tpu_custom_call" | custom-call | flops 99999997952 | bytes 1000000 | tf_op jit(solution)/shard_map/pallas_call | solution.py:442
  478.2 1.2 shard_map.53

commit v5 on v4

--- a/solution.py
+++ b/solution.py
@@ -514,7 +514,7 @@
     _, sub_count, n_row = shard_order.shape
     rows_tile, cols_tile = train_weight.shape
     chunks = rows_tile // LANES if rows_tile % LANES == 0 else 1
-    late = LATE_CHUNKS if chunks > max(LATE_CHUNKS) and lax.axis_size("rep") > 2 else (0, 0)
+    late = LATE_CHUNKS if chunks > max(LATE_CHUNKS) and lax.axis_size("rep") > 3 else (0, 0)
     reorder = (cols_tile // (n_row * sub_count)) % LANES == 0
     tile = train_weight if reorder else ordered_pieces(train_weight, shard_order)
     landed, summed, keep = handed_off(hidden, tile, shard_order, chunks, late, reorder)

time: 480 us -> 480 us (level)
  no operation moved by 1% of the time
where the time goes in v5:
time: 480 us; the launch traced here: 479 us
  Pallas kernels  479 us (100%)
    pallas_call x1, Pallas kernels, handed_off(): pl.pallas_call(functools.partial(handoff_kernel, n_row, n_rep, chunks, la...  454 us
    pallas_call x1, Pallas kernels, late_handoff(): pl.pallas_call(functools.partial(late_kernel, n_row, n_rep, chunks, late)...  13.5 us
    pallas_call x1, Pallas kernels, stored(): pl.pallas_call(store_kernel, out_shape=jax.ShapeDtypeStruct(landed.shape,...  9.84 us

profile of v5, /device:TPU:0, one launch (start us, length us, event | category | flops | bytes accessed | tf_op | source)
XLA Modules:
  0.0 479.4 jit_solution(5384390650577731185)
XLA Ops:
  0.6 454.1 %shard_map.50 = (bf16[7168,2048]{1,0:T(8,128)(2,1)S(1)}, f32[128,2048]{1,0:T(8,128)S(1)}, bf16[768,2048]{1,0:T(8,128)(2,1)S(1)}) custom-call(s32[4,2,4]{2,1,0:T(2,128)} %bitcast.1, bf16[896,4096]{1,0:T(8,128)(2,1)} %tile_ref.1, bf16[128,7168]{1,0:T(8,128)(2,1)} %hidden_hbm.3), custom_call_target="tpu_custom_call" | custom-call | tf_op jit(solution)/shard_map/pallas_call | solution.py:288
  454.8 9.8 %shard_map.51._.early_ref = bf16[7168,2048]{1,0:T(8,128)(2,1)} custom-call(bf16[7168,2048]{1,0:T(8,128)(2,1)S(1)} %get-tuple-element.7.landed_ref), custom_call_target="tpu_custom_call" | custom-call | tf_op jit(solution)/shard_map/pallas_call | solution.py:333
  464.6 13.5 %shard_map.52 = (bf16[768,2048]{1,0:T(8,128)(2,1)S(1)}, f32[128,2048]{1,0:T(8,128)S(1)}) custom-call(bf16[768,2048]{1,0:T(8,128)(2,1)S(1)} %get-tuple-element.8.keep_ref, f32[128,2048]{1,0:T(8,128)S(1)} %get-tuple-element.9.partial_ref, bf16[128,7168]{1,0:T(8,128)(2,1)} %hidden_hbm.3, bf16[7168,2048]{1,0:T(8,128)(2,1)} %shard_map.51._.early_ref), custom_call_target="tpu_custom_call" | custom-call | flops 99999997952 | bytes 1000000 | tf_op jit(solution)/shard_map/pallas_call | solution.py:442
  478.2 1.2 shard_map.53

commit v6 on v5

--- a/solution.py
+++ b/solution.py
@@ -11,6 +11,7 @@
 LANES = 128
 MIB = 1024 * 1024
 LATE_CHUNKS = (1, 6)
+FIRST_CHUNKS = (3, 1)
 
 
 def ordered_pieces(tile, shard_order):
@@ -29,17 +30,215 @@
     return jnp.concatenate(pieces, axis=1)
 
 
+def by_core(pair):
+    return jnp.where(lax.rem(lax.axis_index("col"), 2) == 0, pair[0], pair[1])
+
+
 def late_start(chunks, late):
-    return chunks - jnp.where(lax.rem(lax.axis_index("col"), 2) == 0, late[0], late[1])
+    return chunks - by_core(late)
 
 
 def row_tiles(cols):
     return 256 if cols % 256 == 0 else LANES
 
 
+def step_of(rows):
+    return 16 if rows % 16 == 0 else 8
+
+
+def arrange_rows(order_ref, raw_ref, n_row, first, rows, reorder, shifts, place):
+    r, c = lax.axis_index("row"), lax.axis_index("col")
+    cols = raw_ref.shape[1] // n_row
+    sub_count = order_ref.shape[2]
+    sub_cols = cols // sub_count
+    step = step_of(rows)
+
+    @pl.loop(0, rows // step)
+    def _(i):
+        to = first + i * step
+        at = pl.ds(pl.multiple_of(to, step), step)
+        if reorder:
+            for k in range(sub_count):
+                blocks = [raw_ref[at, pl.ds(j * cols + k * sub_cols, sub_cols)] for j in range(n_row)]
+                for t in shifts:
+                    s = lax.rem(r + t, n_row)
+                    piece = blocks[0]
+                    for j in range(1, n_row):
+                        piece = jnp.where(order_ref[c, s, k] == j, blocks[j], piece)
+                    place(t, to, pl.ds(k * sub_cols, sub_cols), piece)
+        else:
+            for t in shifts:
+                s = lax.rem(r + t, n_row)
+                place(t, to, pl.ds(0, cols), raw_ref[at, pl.ds(pl.multiple_of(s * cols, LANES), cols)])
+
+
+def edges(n_rep):
+    z = lax.axis_index("rep")
+    return z == n_rep - 2, z == 1, z == n_rep - 1, z == 0
+
+
+def pair_barrier(n_rep, above, below):
+    gives_up, gives_down, takes_below, takes_above = edges(n_rep)
+    barrier = pltpu.get_barrier_semaphore()
+
+    @pl.when(gives_up | takes_above)
+    def _():
+        pl.semaphore_signal(barrier, inc=1, device_id=above, device_id_type=MESH)
+
+    @pl.when(gives_down | takes_below)
+    def _():
+        pl.semaphore_signal(barrier, inc=1, device_id=below, device_id_type=MESH)
+
+    return barrier, (gives_up | takes_above).astype(jnp.int32) + (gives_down | takes_below).astype(jnp.int32)
+
+
+def first_kernel(
+    n_row, n_rep, chunks, first, reorder,
+    order_hbm, tile_ref, landed_ref, order_ref, raw_ref, own_ref, order_sem, raw_sem, send_sem, recv_sem,
+):
+    r, c, z = lax.axis_index("row"), lax.axis_index("col"), lax.axis_index("rep")
+    rows = tile_ref.shape[0] // chunks
+    count = by_core(first)
+    gives_up, gives_down, takes_below, takes_above = edges(n_rep)
+    above = (r, c, jnp.minimum(z + 1, n_rep - 1))
+    below = (r, c, jnp.maximum(z - 1, 0))
+    barrier, expected = pair_barrier(n_rep, above, below)
+
+    parts = 4 if rows % 64 == 0 else 1
+    part = rows // parts
+
+    def chunk_of(ref, q, i=None):
+        if i is None:
+            return ref.at[pl.ds(pl.multiple_of(q * rows, 8), rows)]
+        return ref.at[pl.ds(pl.multiple_of(q * rows + i * part, 8), part)]
+
+    def staged(q):
+        return pltpu.make_async_copy(chunk_of(tile_ref, q), chunk_of(raw_ref, q), raw_sem.at[parts + q])
+
+    def staged_part(i):
+        return pltpu.make_async_copy(chunk_of(tile_ref, 0, i), chunk_of(raw_ref, 0, i), raw_sem.at[i])
+
+    def moved(q, target, i=None):
+        return pltpu.make_async_remote_copy(
+            src_ref=chunk_of(own_ref, q, i),
+            dst_ref=chunk_of(landed_ref, q, i),
+            send_sem=send_sem.at[q],
+            recv_sem=recv_sem.at[q],
+            device_id=target,
+            device_id_type=MESH,
+        )
+
+    def place(t, to, span, piece):
+        own_ref[pl.ds(pl.multiple_of(to, 8), step_of(rows)), span] = piece
+
+    gives = gives_up | gives_down
+
+    def arrange(first, height):
+        arrange_rows(order_ref, raw_ref, n_row, first, height, reorder, (0,), place)
+
+    @pl.when(gives)
+    def _():
+        order_copy = pltpu.make_async_copy(order_hbm, order_ref, order_sem)
+        order_copy.start()
+
+        @pl.loop(0, parts)
+        def _(i):
+            staged_part(i).start()
+
+        order_copy.wait()
+        staged_part(0).wait()
+        arrange(0, part)
+
+        @pl.loop(1, count)
+        def _(q):
+            staged(q).start()
+
+    @pl.when(expected > 0)
+    def _():
+        pl.semaphore_wait(barrier, expected)
+
+    def send(q, i=None):
+        @pl.when(gives_up)
+        def _():
+            moved(q, above, i).start()
+
+        @pl.when(gives_down)
+        def _():
+            moved(q, below, i).start()
+
+    @pl.when(gives)
+    def _():
+        send(0, 0)
+
+        @pl.loop(1, parts)
+        def _(i):
+            staged_part(i).wait()
+            arrange(i * part, part)
+
+        @pl.loop(1, parts)
+        def _(i):
+            send(0, i)
+
+        @pl.loop(1, count)
+        def _(q):
+            staged(q).wait()
+            arrange(q * rows, rows)
+
+        @pl.loop(1, count)
+        def _(q):
+            send(q)
+
+        @pl.loop(0, count)
+        def _(q):
+            @pl.when(gives_up)
+            def _():
+                moved(q, above).wait_send()
+
+            @pl.when(gives_down)
+            def _():
+                moved(q, below).wait_send()
+
+    @pl.when(takes_below)
+    def _():
+        @pl.loop(0, count)
+        def _(q):
+            moved(q, below).wait_recv()
+
+    @pl.when(takes_above)
+    def _():
+        @pl.loop(0, count)
+        def _(q):
+            moved(q, above).wait_recv()
+
+
+def first_handoff(tile, order, cols, chunks, first, reorder):
+    n_row, n_rep = lax.axis_size("row"), lax.axis_size("rep")
+    slots = max(first)
+    height = slots * (tile.shape[0] // chunks)
+    dma = pltpu.SemaphoreType.DMA
+    return pl.pallas_call(
+        functools.partial(first_kernel, n_row, n_rep, chunks, first, reorder),
+        out_shape=pltpu.VMEM((height, cols), tile.dtype),
+        in_specs=[hbm(), hbm()],
+        out_specs=vmem(),
+        scratch_shapes=[
+            pltpu.SMEM(order.shape, order.dtype),
+            pltpu.VMEM((height, tile.shape[1]), tile.dtype),
+            pltpu.VMEM((height, cols), tile.dtype),
+            dma,
+            dma((slots + 4,)),
+            dma((slots,)),
+            dma((slots,)),
+        ],
+        compiler_params=pltpu.CompilerParams(
+            collective_id=2, has_side_effects=True, vmem_limit_bytes=6 * MIB
+        ),
+    )(in_hbm(order), in_hbm(tile))
+
+
 def handoff_kernel(
-    n_row, n_rep, chunks, late, reorder,
-    order_hbm, tile_ref, hidden_hbm, full_ref, projected_ref, keep_ref,
+    n_row, n_rep, chunks, late, first, reorder,
+    order_hbm, tile_ref, hidden_hbm, landed_ref, full_ref, projected_ref, keep_ref,
     order_ref, raw_ref, away_ref, hidden_ref, order_sem, raw_sem, hidden_sem, y_send, y_recv, z_recv, up_send, down_send,
 ):
     r, c, z = lax.axis_index("row"), lax.axis_index("col"), lax.axis_index("rep")
@@ -52,6 +251,9 @@
     per_level = n_row * chunks
     mine = z * n_row + r
     kept = (n_row - 1) * chunks + late_start(chunks, late)
+    gives_up, gives_down, takes_below, takes_above = edges(n_rep)
+    ahead = by_core(first)
+    up_from, down_from = jnp.where(gives_up, ahead, 0), jnp.where(gives_down, ahead, 0)
 
     barrier = pltpu.get_barrier_semaphore()
     for t in range(1, n_row):
@@ -76,37 +278,17 @@
     order_copy.start()
     staged(0).start()
 
-    sub_count = order_ref.shape[2]
-    sub_cols = cols // sub_count
-    step = 16 if rows % 16 == 0 else 8
+    def place(t, to, span, piece):
+        if t == 0:
+            full_ref[pl.ds(pl.multiple_of(mine * rows_tile + to, 8), step), span] = piece
+        else:
+            away_ref[t - 1, pl.ds(pl.multiple_of(to, 8), step), span] = piece
+
+    step = step_of(rows)
 
     def arrange(q):
         staged(q).wait()
-
-        @pl.loop(0, rows // step)
-        def _(i):
-            at = pl.ds(pl.multiple_of(q * rows + i * step, step), step)
-            to = pl.ds(pl.multiple_of(mine * rows_tile + q * rows + i * step, step), step)
-
-            def place(t, span, piece):
-                if t == 0:
-                    full_ref[to, span] = piece
-                else:
-                    away_ref[t - 1, at, span] = piece
-
-            if reorder:
-                for k in range(sub_count):
-                    blocks = [raw_ref[at, pl.ds(j * cols + k * sub_cols, sub_cols)] for j in range(n_row)]
-                    for t in range(n_row):
-                        s = lax.rem(r + t, n_row)
-                        piece = blocks[0]
-                        for j in range(1, n_row):
-                            piece = jnp.where(order_ref[c, s, k] == j, blocks[j], piece)
-                        place(t, pl.ds(k * sub_cols, sub_cols), piece)
-            else:
-                for t in range(n_row):
-                    s = lax.rem(r + t, n_row)
-                    place(t, pl.ds(0, cols), raw_ref[at, pl.ds(pl.multiple_of(s * cols, LANES), cols)])
+        arrange_rows(order_ref, raw_ref, n_row, q * rows, rows, reorder, range(n_row), place)
 
     def along_row(t, q, outward):
         peer = lax.rem(r + t, n_row)
@@ -130,12 +312,12 @@
             device_id_type=MESH,
         )
 
-    def forward(block, q):
-        @pl.when(has_up)
+    def forward(block, q, up=True, down=True):
+        @pl.when(has_up & up)
         def _():
             along_rep(block, q, up_send, above).start()
 
-        @pl.when(has_down)
+        @pl.when(has_down & down)
         def _():
             along_rep(block, q, down_send, below).start()
 
@@ -156,7 +338,7 @@
             multiply(pl.multiple_of(block * rows_tile + q * rows, LANES), rows, False)
 
     def send_own(q):
-        forward(mine, q)
+        forward(mine, q, q >= up_from, q >= down_from)
         for t in range(1, n_row):
             along_row(t, q, True).start()
 
@@ -205,7 +387,20 @@
     def arrived(d, level, i, sems, target, onward):
         block, q = block_of(level, i)
         copy = along_rep(block, q, sems, target)
-        copy.wait_recv()
+        taken = (d == 1) & (i < ahead) & jnp.logical_not(onward)
+
+        @pl.when(jnp.logical_not(taken))
+        def _():
+            copy.wait_recv()
+
+        if max(first):
+
+            @pl.when(taken)
+            def _():
+                full_ref[pl.ds(pl.multiple_of(block * rows_tile + q * rows, LANES), rows), :] = landed_ref[
+                    pl.ds(pl.multiple_of(jnp.minimum(q, max(first) - 1) * rows, LANES), rows), :
+                ]
+
         deferred = (d == n_rep - 2) & (i >= kept)
 
         @pl.when(onward & jnp.logical_not(deferred))
@@ -246,8 +441,8 @@
         for t in range(1, n_row):
             along_row(t, q, True).wait_send()
 
-    def drain(level, sent, sems, target):
-        @pl.loop(0, sent)
+    def drain(level, begin, sent, sems, target):
+        @pl.loop(begin, sent)
         def _(i):
             block, q = block_of(level, i)
             along_rep(block, q, sems, target).wait_send()
@@ -256,13 +451,13 @@
     def _():
         @pl.loop(0, z + 1)
         def _(level):
-            drain(level, jnp.where((level == 0) & (z + 1 == n_rep - 1), kept, per_level), up_send, above)
+            drain(level, jnp.where(level == z, up_from, 0), jnp.where((level == 0) & gives_up, kept, per_level), up_send, above)
 
     @pl.when(has_down)
     def _():
         @pl.loop(z, n_rep)
         def _(level):
-            drain(level, jnp.where((level == n_rep - 1) & (z == 1), kept, per_level), down_send, below)
+            drain(level, jnp.where(level == z, down_from, 0), jnp.where((level == n_rep - 1) & gives_down, kept, per_level), down_send, below)
 
 
 def vmem():
@@ -277,22 +472,25 @@
     return pl.BlockSpec(memory_space=pltpu.HBM)
 
 
-def handed_off(hidden, tile, shard_order, chunks, late, reorder):
+def handed_off(hidden, tile, order, chunks, late, first, reorder):
     n_row, n_rep = lax.axis_size("row"), lax.axis_size("rep")
     rows_tile, cols_tile = tile.shape
     cols = cols_tile // n_row
     every = n_rep * n_row * chunks
-    order = jnp.swapaxes(shard_order, 1, 2)
+    if max(first):
+        landed = first_handoff(tile, order, cols, chunks, first, reorder)
+    else:
+        landed = jnp.zeros((8, cols), tile.dtype)
     dma = pltpu.SemaphoreType.DMA
     height = n_rep * n_row * rows_tile
     return pl.pallas_call(
-        functools.partial(handoff_kernel, n_row, n_rep, chunks, late, reorder),
+        functools.partial(handoff_kernel, n_row, n_rep, chunks, late, first, reorder),
         out_shape=(
             pltpu.VMEM((height, cols), tile.dtype),
             pltpu.VMEM((hidden.shape[0], cols), jnp.float32),
             pltpu.VMEM((max(8, max(late) * (rows_tile // chunks)), cols), tile.dtype),
         ),
-        in_specs=[hbm(), hbm(), hbm()],
+        in_specs=[hbm(), hbm(), hbm(), vmem()],
         out_specs=(vmem(),) * 3,
         scratch_shapes=[
             pltpu.SMEM(order.shape, order.dtype),
@@ -311,7 +509,7 @@
         compiler_params=pltpu.CompilerParams(
             collective_id=0, has_side_effects=True, vmem_limit_bytes=14 * MIB
         ),
-    )(in_hbm(order), in_hbm(tile), in_hbm(hidden))
+    )(in_hbm(order), in_hbm(tile), in_hbm(hidden), landed)
 
 
 def store_kernel(landed_ref, served_ref, sem):
@@ -351,22 +549,12 @@
     first = late_start(chunks, late)
     other = lax.rem(r + 1, n_row)
     lowest, highest = other, (n_rep - 1) * n_row + other
-    gives_up, gives_down = z == n_rep - 2, z == 1
-    takes_below, takes_above = z == n_rep - 1, z == 0
+    gives_up, gives_down, takes_below, takes_above = edges(n_rep)
     above = (r, c, jnp.minimum(z + 1, n_rep - 1))
     below = (r, c, jnp.maximum(z - 1, 0))
 
-    barrier = pltpu.get_barrier_semaphore()
-
-    @pl.when(gives_up | takes_above)
-    def _():
-        pl.semaphore_signal(barrier, inc=1, device_id=above, device_id_type=MESH)
-
-    @pl.when(gives_down | takes_below)
-    def _():
-        pl.semaphore_signal(barrier, inc=1, device_id=below, device_id_type=MESH)
-
-    pl.semaphore_wait(barrier, (gives_up | takes_above).astype(jnp.int32) + (gives_down | takes_below).astype(jnp.int32))
+    barrier, expected = pair_barrier(n_rep, above, below)
+    pl.semaphore_wait(barrier, expected)
 
     def moved(q, target):
         slot = q - (chunks - slots)
@@ -514,10 +702,12 @@
     _, sub_count, n_row = shard_order.shape
     rows_tile, cols_tile = train_weight.shape
     chunks = rows_tile // LANES if rows_tile % LANES == 0 else 1
-    late = LATE_CHUNKS if chunks > max(LATE_CHUNKS) and lax.axis_size("rep") > 3 else (0, 0)
+    split = chunks > max(LATE_CHUNKS + FIRST_CHUNKS) and lax.axis_size("rep") > 3
+    late = LATE_CHUNKS if split else (0, 0)
+    first = FIRST_CHUNKS if split else (0, 0)
     reorder = (cols_tile // (n_row * sub_count)) % LANES == 0
     tile = train_weight if reorder else ordered_pieces(train_weight, shard_order)
-    landed, summed, keep = handed_off(hidden, tile, shard_order, chunks, late, reorder)
+    landed, summed, keep = handed_off(hidden, tile, jnp.swapaxes(shard_order, 1, 2), chunks, late, first, reorder)
     served = stored(landed)
     if max(late) == 0:
         return served, summed

time: 480 us -> 479 us (level)
    pallas_call x0 -> x1, Pallas kernels: none -> 35.7 us  [first_handoff(): pl.pallas_call(functools.partial(first_kernel, n_row, n_rep, chunks, firs...]
    pallas_call x1, Pallas kernels: 454 us -> 419 us  [handed_off(): pl.pallas_call(functools.partial(handoff_kernel, n_row, n_rep, chunks, la...]
where the time goes in v6:
time: 479 us
  Pallas kernels  478 us (100%)
    pallas_call x1, Pallas kernels, handed_off(): pl.pallas_call(functools.partial(handoff_kernel, n_row, n_rep, chunks, la...  419 us
    pallas_call x1, Pallas kernels, first_handoff(): pl.pallas_call(functools.partial(first_kernel, n_row, n_rep, chunks, firs...  35.7 us
    pallas_call x1, Pallas kernels, late_handoff(): pl.pallas_call(functools.partial(late_kernel, n_row, n_rep, chunks, late)...  12.5 us
    pallas_call x1, Pallas kernels, stored(): pl.pallas_call(store_kernel, out_shape=jax.ShapeDtypeStruct(landed.shape,...  9.84 us

profile of v6, /device:TPU:0, one launch (start us, length us, event | category | flops | bytes accessed | tf_op | source)
XLA Modules:
  0.0 478.9 jit_solution(16686738694235865128)
XLA Ops:
  0.6 35.7 %shard_map.50.landed_ref = bf16[384,2048]{1,0:T(8,128)(2,1)S(1)} custom-call(s32[4,2,4]{2,1,0:T(2,128)} %bitcast.1, bf16[896,4096]{1,0:T(8,128)(2,1)} %tile_ref.3), custom_call_target="tpu_custom_call" | custom-call | tf_op jit(solution)/shard_map/pallas_call | solution.py:219
  36.3 419.1 %shard_map.51 = (bf16[7168,2048]{1,0:T(8,128)(2,1)S(1)}, f32[128,2048]{1,0:T(8,128)S(1)}, bf16[768,2048]{1,0:T(8,128)(2,1)S(1)}) custom-call(s32[4,2,4]{2,1,0:T(2,128)} %bitcast.2, bf16[896,4096]{1,0:T(8,128)(2,1)} %tile_ref.3, bf16[128,7168]{1,0:T(8,128)(2,1)} %hidden_hbm.3, bf16[384,2048]{1,0:T(8,128)(2,1)S(1)} %shard_map.50.landed_ref), custom_call_target="tpu_custom_call" | custom-call | tf_op jit(solution)/shard_map/pallas_call | solution.py:486
  455.4 9.8 %shard_map.52._.early_ref = bf16[7168,2048]{1,0:T(8,128)(2,1)} custom-call(bf16[7168,2048]{1,0:T(8,128)(2,1)S(1)} %get-tuple-element.7.landed_ref), custom_call_target="tpu_custom_call" | custom-call | tf_op jit(solution)/shard_map/pallas_call | solution.py:531
  465.2 12.5 %shard_map.53 = (bf16[768,2048]{1,0:T(8,128)(2,1)S(1)}, f32[128,2048]{1,0:T(8,128)S(1)}) custom-call(bf16[768,2048]{1,0:T(8,128)(2,1)S(1)} %get-tuple-element.8.keep_ref, f32[128,2048]{1,0:T(8,128)S(1)} %get-tuple-element.9.partial_ref, bf16[128,7168]{1,0:T(8,128)(2,1)} %hidden_hbm.3, bf16[7168,2048]{1,0:T(8,128)(2,1)} %shard_map.52._.early_ref), custom_call_target="tpu_custom_call" | custom-call | flops 99999997952 | bytes 1000000 | tf_op jit(solution)/shard_map/pallas_call | solution.py:630
  477.7 1.2 shard_map.54

commit v7 on v6

--- a/solution.py
+++ b/solution.py
@@ -11,7 +11,7 @@
 LANES = 128
 MIB = 1024 * 1024
 LATE_CHUNKS = (1, 6)
-FIRST_CHUNKS = (3, 1)
+FIRST_CHUNKS = (1, 3)
 
 
 def ordered_pieces(tile, shard_order):

time: 479 us -> 479 us (level)
    pallas_call x1, Pallas kernels: 35.7 us -> 17 us  [first_handoff(): pl.pallas_call(functools.partial(first_kernel, n_row, n_rep, chunks, firs...]
    pallas_call x1, Pallas kernels: 419 us -> 436 us  [handed_off(): pl.pallas_call(functools.partial(handoff_kernel, n_row, n_rep, chunks, la...]
where the time goes in v7:
time: 479 us
  Pallas kernels  478 us (100%)
    pallas_call x1, Pallas kernels, handed_off(): pl.pallas_call(functools.partial(handoff_kernel, n_row, n_rep, chunks, la...  436 us
    pallas_call x1, Pallas kernels, first_handoff(): pl.pallas_call(functools.partial(first_kernel, n_row, n_rep, chunks, firs...  17 us
    pallas_call x1, Pallas kernels, late_handoff(): pl.pallas_call(functools.partial(late_kernel, n_row, n_rep, chunks, late)...  13.8 us
    pallas_call x1, Pallas kernels, stored(): pl.pallas_call(store_kernel, out_shape=jax.ShapeDtypeStruct(landed.shape,...  9.84 us

profile of v7, /device:TPU:0, one launch (start us, length us, event | category | flops | bytes accessed | tf_op | source)
XLA Modules:
  0.0 478.9 jit_solution(6718888881599785665)
XLA Ops:
  0.6 17.0 %shard_map.50.landed_ref = bf16[384,2048]{1,0:T(8,128)(2,1)S(1)} custom-call(s32[4,2,4]{2,1,0:T(2,128)} %bitcast.1, bf16[896,4096]{1,0:T(8,128)(2,1)} %tile_ref.3), custom_call_target="tpu_custom_call" | custom-call | tf_op jit(solution)/shard_map/pallas_call | solution.py:219
  17.6 436.5 %shard_map.51 = (bf16[7168,2048]{1,0:T(8,128)(2,1)S(1)}, f32[128,2048]{1,0:T(8,128)S(1)}, bf16[768,2048]{1,0:T(8,128)(2,1)S(1)}) custom-call(s32[4,2,4]{2,1,0:T(2,128)} %bitcast.2, bf16[896,4096]{1,0:T(8,128)(2,1)} %tile_ref.3, bf16[128,7168]{1,0:T(8,128)(2,1)} %hidden_hbm.3, bf16[384,2048]{1,0:T(8,128)(2,1)S(1)} %shard_map.50.landed_ref), custom_call_target="tpu_custom_call" | custom-call | tf_op jit(solution)/shard_map/pallas_call | solution.py:486
  454.1 9.8 %shard_map.52._.early_ref = bf16[7168,2048]{1,0:T(8,128)(2,1)} custom-call(bf16[7168,2048]{1,0:T(8,128)(2,1)S(1)} %get-tuple-element.7.landed_ref), custom_call_target="tpu_custom_call" | custom-call | tf_op jit(solution)/shard_map/pallas_call | solution.py:531
  464.0 13.8 %shard_map.53 = (bf16[768,2048]{1,0:T(8,128)(2,1)S(1)}, f32[128,2048]{1,0:T(8,128)S(1)}) custom-call(bf16[768,2048]{1,0:T(8,128)(2,1)S(1)} %get-tuple-element.8.keep_ref, f32[128,2048]{1,0:T(8,128)S(1)} %get-tuple-element.9.partial_ref, bf16[128,7168]{1,0:T(8,128)(2,1)} %hidden_hbm.3, bf16[7168,2048]{1,0:T(8,128)(2,1)} %shard_map.52._.early_ref), custom_call_target="tpu_custom_call" | custom-call | flops 99999997952 | bytes 1000000 | tf_op jit(solution)/shard_map/pallas_call | solution.py:630
  477.7 1.2 shard_map.54
